TPU v7x, 32 devices: a whole 2x2x4 slice. The times are simulated.
32 devices in a mesh: tok: 4 (over y, x), hid: 2 (over core), voc: 4 (over z).
Axes of the slice: x: 2, y: 2, z: 4, core: 2. Of those that a mesh axis runs over, the one named last changes fastest.
Arguments:
- student_hidden: bfloat16 [512, 8192], P('tok', ('hid', 'voc')), may hold values from -8 to 8
- teacher_hidden: bfloat16 [512, 16384], P('tok', ('hid', 'voc')), may hold values from -8 to 8
- student_head: bfloat16 [8192, 2048], P('hid', 'voc'), may hold values from -2 to 2
- teacher_head: bfloat16 [16384, 2048], P('hid', 'voc'), may hold values from -2 to 2
- loss_weight: float32 [512], P('tok'), may hold values from 128 to 1024
Outputs:
- grad_hidden: bfloat16 [512, 8192], P('tok', ('hid', 'voc'))
- mean_loss: float32 [], replicated
All inputs are finite; a program needn't handle non-finite values.
Results may differ from a plain program's by a relative error of at most 0.001.
The roundings to bfloat16 on the way count: a program that leaves them out, or rounds other values in their place, can miss the bound.
Values may be sent and summed in bfloat16 or wider, within the bound.
A program may use at most 64 MiB of HBM per device.

v0:
```python
import jax
import jax.numpy as jnp
from jax import lax
from jax.sharding import PartitionSpec as P


def divergence_terms(student_logits, teacher_logits, weights):
    differences = teacher_logits - student_logits
    peak_student, peak_teacher = lax.pmax(
        (jnp.max(student_logits, axis=1), jnp.max(teacher_logits, axis=1)), "voc"
    )
    scaled_student = jnp.exp(student_logits - peak_student[:, None])
    scaled_teacher = jnp.exp(teacher_logits - peak_teacher[:, None])
    total_student, total_teacher, cross_sum = lax.psum(
        (
            jnp.sum(scaled_student, axis=1),
            jnp.sum(scaled_teacher, axis=1),
            jnp.sum(scaled_teacher * differences, axis=1),
        ),
        "voc",
    )
    student_lse = peak_student + jnp.log(total_student)
    teacher_lse = peak_teacher + jnp.log(total_teacher)
    divergence = cross_sum / total_teacher - teacher_lse + student_lse
    prob_gap = jnp.exp(student_logits - student_lse[:, None]) - jnp.exp(
        teacher_logits - teacher_lse[:, None]
    )
    scaled_gap = (weights[:, None] * prob_gap).astype(jnp.bfloat16)
    return (divergence, scaled_gap)


def shards(student_hidden, teacher_hidden, student_head, teacher_head, loss_weight):
    student_block, teacher_block = (
        lax.all_gather(student_hidden, "voc", axis=1, tiled=True),
        lax.all_gather(teacher_hidden, "voc", axis=1, tiled=True),
    )
    vocab_local = student_head.shape[1]
    row_count = student_block.shape[0] // lax.axis_size("hid")
    joined = lax.psum_scatter(
        jnp.concatenate(
            [
                jnp.dot(student_block, student_head, preferred_element_type=jnp.float32),
                jnp.dot(teacher_block, teacher_head, preferred_element_type=jnp.float32),
            ],
            axis=1,
        ),
        "hid",
        scatter_dimension=0,
        tiled=True,
    )
    student_logits = joined[:, :vocab_local]
    teacher_logits = joined[:, vocab_local:]
    weights = lax.dynamic_slice_in_dim(loss_weight, lax.axis_index("hid") * row_count, row_count)
    divergence, scaled_gap = divergence_terms(student_logits, teacher_logits, weights)
    token_total = loss_weight.shape[0] * lax.axis_size("tok")
    loss_total = lax.psum(jnp.sum(divergence), ("tok", "hid"))
    grad_terms = lax.dot_general(
        lax.all_gather(scaled_gap, "hid", axis=0, tiled=True),
        student_head,
        (((1,), (1,)), ((), ())),
        preferred_element_type=jnp.float32,
    )
    grad_hidden = lax.psum_scatter(grad_terms, "voc", scatter_dimension=1, tiled=True).astype(
        jnp.bfloat16
    )
    mean_loss = loss_total / token_total
    return (grad_hidden, mean_loss)


def solution(mesh):
    placed = (
        P("tok", ("hid", "voc")),
        P("tok", ("hid", "voc")),
        P("hid", "voc"),
        P("hid", "voc"),
        P("tok"),
    )
    return jax.shard_map(
        shards,
        mesh=mesh,
        in_specs=placed,
        out_specs=(P("tok", ("hid", "voc")), P()),
        check_vma=False,
    )
```

profile of v0, /device:TPU:0, one launch (start us, length us, event | category | flops | bytes accessed | tf_op | source)
XLA Modules:
  0.0 184.0 jit_solution(341071947678527449)
XLA Ops:
  7.2 0.0 all-gather.3.cloned.1.call-start
  7.2 0.7 all-gather.3.cloned.1.call-update
  7.9 0.0 all-gather.5.cloned.1.call-start
  7.9 0.7 all-gather.5.cloned.1.call-update
  8.6 0.0 reduce-scatter.3.cloned.1.call-start
  8.7 31.6 %all-gather.3.cloned.1.call-done = bf16[128,4096]{1,0:T(8,128)(2,1)} async-done(((bf16[128,1024]{1,0:T(8,128)(2,1)}), bf16[128,4096]{1,0:T(8,128)(2,1)}) %all-gather.3.cloned.1.call-update) | async-done | bytes 1048592 | tf_op jit(solution)/shard_map/all_gather | solution.py:34
  40.3 3.2 %fusion.1 = f32[128,512]{1,0:T(8,128)S(1)} fusion(bf16[128,4096]{1,0:T(8,128)(2,1)} %all-gather.3.cloned.1.call-done, bf16[4096,512]{1,0:T(8,128)(2,1)} %param.7), kind=kOutput, calls=%fused_computation.11 | convolution fusion | flops 536870912 | bytes 5505024 | tf_op jit(solution)/shard_map/dot_general | solution.py:42
  43.5 0.0 copy-start
  43.5 43.4 %all-gather.5.cloned.1.call-done = bf16[128,8192]{1,0:T(8,128)(2,1)} async-done(((bf16[128,2048]{1,0:T(8,128)(2,1)}), bf16[128,8192]{1,0:T(8,128)(2,1)}) %all-gather.5.cloned.1.call-update) | async-done | bytes 2097168 | tf_op jit(solution)/shard_map/all_gather | solution.py:35
  86.9 5.3 %fusion.2 = f32[128,512]{1,0:T(8,128)S(1)} fusion(bf16[128,8192]{1,0:T(8,128)(2,1)} %all-gather.5.cloned.1.call-done, bf16[8192,512]{1,0:T(8,128)(2,1)} %param.8), kind=kOutput, calls=%fused_computation.12 | convolution fusion | flops 1073741824 | bytes 10747904 | tf_op jit(solution)/shard_map/dot_general | solution.py:43
  92.2 0.8 pad_maximum_fusion
  93.0 0.0 reduce-scatter.3.cloned.1.call-update
  93.1 0.0 reduce-scatter.5.cloned.1.call-start
  93.1 0.0 copy-done
  93.1 0.1 dynamic_slice.3
  93.2 6.7 %reduce-scatter.3.cloned.1.call-done = f32[64,1024]{1,0:T(8,128)} async-done(((f32[128,1024]{1,0:T(8,128)}), f32[64,1024]{1,0:T(8,128)}) %reduce-scatter.3.cloned.1.call-update) | async-done | bytes 262160 | tf_op jit(solution)/shard_map/reduce_scatter | solution.py:39
  99.9 1.1 slice_reduce_fusion.1
  101.0 11.9 %all-reduce.1 = (f32[64]{0:T(128)S(1)}, f32[64]{0:T(128)S(1)}) all-reduce(f32[64]{0:T(128)S(1)} %get-tuple-element.6, f32[64]{0:T(128)S(1)} %get-tuple-element.5), channel_id=1, replica_groups=mesh['tok'=4,'hid'=2,'voc'=4] {'voc'}, use_global_device_ids=true, to_apply=%region_6.0 | all-reduce | flops 128 | bytes 1024 | tf_op jit(solution)/shard_map/pmax | solution.py:9
  112.9 1.2 multiply_reduce_fusion
  114.1 8.4 %all-reduce = (f32[64]{0:T(128)S(1)}, f32[64]{0:T(128)S(1)}, f32[64]{0:T(128)S(1)}) all-reduce(f32[64]{0:T(128)S(1)} %get-tuple-element.3, f32[64]{0:T(128)S(1)} %get-tuple-element.4, f32[64]{0:T(128)S(1)} %get-tuple-element.2), channel_id=1, replica_groups=mesh['tok'=4,'hid'=2,'voc'=4] {'voc'}, use_global_device_ids=true, to_apply=%region_8.0 | all-reduce | flops 192 | bytes 1536 | tf_op jit(solution)/shard_map/psum | solution.py:14
  122.5 0.6 add_reduce_fusion
  123.1 1.1 multiply_convert_fusion
  124.2 1.9 %all_gather.11 = bf16[128,512]{1,0:T(8,128)(2,1)S(1)} all-gather(bf16[64,512]{1,0:T(8,128)(2,1)S(1)} %multiply_convert_fusion), channel_id=1, replica_groups=mesh['tok'=4,'hid'=2,'voc'=4] {'hid'}, dimensions={0}, use_global_device_ids=true | all-gather | bytes 196608 | tf_op jit(solution)/shard_map/all_gather | solution.py:58
  126.1 5.0 %fusion.3 = f32[128,4096]{1,0:T(8,128)} fusion(bf16[128,512]{1,0:T(8,128)(2,1)S(1)} %all_gather.11, bf16[4096,512]{1,0:T(8,128)(2,1)} %param.7), kind=kOutput, calls=%fused_computation.13 | convolution fusion | flops 536870912 | bytes 6422528 | tf_op jit(solution)/shard_map/dot_general | solution.py:57
  131.1 0.0 reduce-scatter.5.cloned.1.call-update
  131.1 15.0 %psum.31 = f32[]{:T(128)} all-reduce(f32[]{:T(128)} %get-tuple-element.12), channel_id=1, replica_groups=mesh['tok'=4,'hid'=2,'voc'=4] {'tok','hid'}, use_global_device_ids=true, to_apply=%region_13.0 | all-reduce | flops 1 | bytes 8 | tf_op jit(solution)/shard_map/psum | solution.py:56
  146.8 27.8 %reduce-scatter.5.cloned.1.call-done = f32[128,1024]{1,0:T(8,128)} async-done(((f32[128,4096]{1,0:T(8,128)}), f32[128,1024]{1,0:T(8,128)}) %reduce-scatter.5.cloned.1.call-update) | async-done | bytes 524304 | tf_op jit(solution)/shard_map/reduce_scatter | solution.py:63
  174.5 1.8 convert_element_type.7
Async XLA Ops:
  7.2 33.1 %all-gather.3.cloned.1.call-start = ((), (), s32[]{:S(2)}) async-start(), calls=%async_computation.2 | async-start | bytes 1310720 | tf_op jit(solution)/shard_map/all_gather | solution.py:34
  7.9 79.0 %all-gather.5.cloned.1.call-start = ((), (), s32[]{:S(2)}) async-start(), calls=%async_computation.3 | async-start | bytes 2621440 | tf_op jit(solution)/shard_map/all_gather | solution.py:35
  8.6 91.3 %reduce-scatter.3.cloned.1.call-start = ((), (), s32[]{:S(2)}) async-start(), calls=%async_computation.4 | async-start | bytes 786432 | tf_op jit(solution)/shard_map/reduce_scatter | solution.py:39
  43.5 49.6 %copy-start = (f32[128]{0:T(128)S(1)}, f32[128]{0:T(128)}, u32[]{:S(2)}) copy-start(f32[128]{0:T(128)} %param.9) | copy-start | bytes 1540
  93.1 81.5 %reduce-scatter.5.cloned.1.call-start = ((), (), s32[]{:S(2)}) async-start(), calls=%async_computation.5 | async-start | bytes 2621440 | tf_op jit(solution)/shard_map/reduce_scatter | solution.py:63
Sparse Core Ops, SparseCore 0:
  9.5 30.6 all-gather.2
  41.8 45.0 all-gather.4
  93.2 6.7 reduce-scatter.2
  131.3 43.2 reduce-scatter.4
where the time goes:
time: 184 us
  waiting for transfers between devices  111 us (60%)
  blocking collectives  37.2 us (20%)
  between operations  15.6 us (8%)
  matrix products  13.5 us (7%)
  other arithmetic  6.6 us (4%)
    all_gather x1, waiting for transfers between devices, shards(): lax.all_gather(teacher_hidden, 'voc', axis=1, tiled=True)  43.4 us
    all_gather x1, waiting for transfers between devices, shards(): lax.all_gather(student_hidden, 'voc', axis=1, tiled=True)  31.6 us
    reduce_scatter x1, waiting for transfers between devices, shards(): lax.psum_scatter(grad_terms, 'voc', scatter_dimension=1, tiled=True)  27.8 us
    psum x1, blocking collectives, shards(): loss_total = lax.psum(jnp.sum(divergence), ('tok', 'hid'))  15 us
    pmax x1, blocking collectives, divergence_terms(): lax.pmax((jnp.max(student_logits, axis=1), jnp.max(teacher_logits, axis=1...  11.9 us
    psum x1, blocking collectives, divergence_terms(): lax.psum((jnp.sum(scaled_student, axis=1), jnp.sum(scaled_teacher, axis=1...  8.37 us
    reduce_scatter x1, waiting for transfers between devices, shards(): lax.psum_scatter(jnp.concatenate([jnp.dot(student_block, student_head, pr...  6.73 us
    dot_general x1, matrix products, shards(): jnp.dot(teacher_block, teacher_head, preferred_element_type=jnp.float32)  5.27 us
  transfers between devices with their start and end apart: 4, of which 4 were waited for; matrix products, arithmetic and copies ran while one was open for 2% of the time, Pallas kernels for 0%

commit v1 on v0

--- a/solution.py
+++ b/solution.py
@@ -32,7 +32,7 @@
 def shards(student_hidden, teacher_hidden, student_head, teacher_head, loss_weight):
     student_block, teacher_block = (
         lax.all_gather(student_hidden, "voc", axis=1, tiled=True),
-        lax.all_gather(teacher_hidden, "voc", axis=1, tiled=True),
+        jnp.concatenate(lax.all_gather(teacher_hidden, "voc"), axis=1),
     )
     vocab_local = student_head.shape[1]
     row_count = student_block.shape[0] // lax.axis_size("hid")

time: 184 us -> 187 us (1.016)
  local copies, waits for them, and re-layouts: 0.08 us -> 3.11 us
    reshape x0 -> x1, local copies, waits for them, and re-layouts: none -> 3.03 us  [shards(): jnp.concatenate(lax.all_gather(teacher_hidden, 'voc'), axis=1)]
where the time goes in v1:
time: 187 us; the launch traced here: 186 us
  waiting for transfers between devices  111 us (59%)
  blocking collectives  37.2 us (20%)
  between operations  15.6 us (8%)
  matrix products  12.9 us (7%)
  other arithmetic  6.6 us (4%)
  local copies, waits for them, and re-layouts  3.11 us (2%)
    all_gather x1, waiting for transfers between devices, shards(): lax.all_gather(teacher_hidden, 'voc')  43.4 us
    all_gather x1, waiting for transfers between devices, shards(): lax.all_gather(student_hidden, 'voc', axis=1, tiled=True)  31.6 us
    reduce_scatter x1, waiting for transfers between devices, shards(): lax.psum_scatter(grad_terms, 'voc', scatter_dimension=1, tiled=True)  27.8 us
    psum x1, blocking collectives, shards(): loss_total = lax.psum(jnp.sum(divergence), ('tok', 'hid'))  15 us
    pmax x1, blocking collectives, divergence_terms(): lax.pmax((jnp.max(student_logits, axis=1), jnp.max(teacher_logits, axis=1...  11.9 us
    psum x1, blocking collectives, divergence_terms(): lax.psum((jnp.sum(scaled_student, axis=1), jnp.sum(scaled_teacher, axis=1...  8.37 us
    reduce_scatter x1, waiting for transfers between devices, shards(): lax.psum_scatter(jnp.concatenate([jnp.dot(student_block, student_head, pr...  6.73 us
    dot_general x1, matrix products, shards(): lax.dot_general(lax.all_gather(scaled_gap, 'hid', axis=0, tiled=True), st...  5.01 us
  transfers between devices with their start and end apart: 4, of which 4 were waited for; matrix products, arithmetic and copies ran while one was open for 2% of the time, Pallas kernels for 0%

profile of v1, /device:TPU:0, one launch (start us, length us, event | category | flops | bytes accessed | tf_op | source)
XLA Modules:
  0.0 186.4 jit_solution(15193968785499936180)
XLA Ops:
  7.2 0.0 all-gather.4.cloned.1.call-start
  7.2 0.7 all-gather.4.cloned.1.call-update
  7.9 0.0 all-gather.6.cloned.1.call-start
  7.9 0.7 all-gather.6.cloned.1.call-update
  8.6 0.0 reduce-scatter.3.cloned.1.call-start
  8.7 31.6 %all-gather.4.cloned.1.call-done = bf16[128,4096]{1,0:T(8,128)(2,1)} async-done(((bf16[128,1024]{1,0:T(8,128)(2,1)}), bf16[128,4096]{1,0:T(8,128)(2,1)}) %all-gather.4.cloned.1.call-update) | async-done | bytes 1048592 | tf_op jit(solution)/shard_map/all_gather | solution.py:34
  40.3 3.2 %fusion.1 = f32[128,512]{1,0:T(8,128)S(1)} fusion(bf16[128,4096]{1,0:T(8,128)(2,1)} %all-gather.4.cloned.1.call-done, bf16[4096,512]{1,0:T(8,128)(2,1)} %param.7), kind=kOutput, calls=%fused_computation.11 | convolution fusion | flops 536870912 | bytes 5505024 | tf_op jit(solution)/shard_map/dot_general | solution.py:42
  43.5 43.4 %all-gather.6.cloned.1.call-done = bf16[512,2048]{1,0:T(8,128)(2,1)} async-done(((bf16[128,2048]{1,0:T(8,128)(2,1)}), bf16[512,2048]{1,0:T(8,128)(2,1)}) %all-gather.6.cloned.1.call-update) | async-done | bytes 2097168 | tf_op jit(solution)/shard_map/all_gather | solution.py:35
  86.9 3.0 %copy.7 = bf16[128,4,2048]{0,2,1:T(8,128)(2,1)S(1)} copy(bf16[128,4,2048]{2,0,1:T(8,128)(2,1)} %bitcast.11) | data formatting | bytes 4194304 | tf_op jit(solution)/shard_map/reshape | solution.py:35
  90.0 0.0 copy-start
  90.0 4.7 %fusion.2 = f32[128,512]{1,0:T(8,128)S(1)} fusion(bf16[128,8192]{0,1:T(8,128)(2,1)S(1)} %bitcast.10, bf16[8192,512]{1,0:T(8,128)(2,1)} %param.8), kind=kOutput, calls=%fused_computation.12 | convolution fusion | flops 1073741824 | bytes 10747904 | tf_op jit(solution)/shard_map/dot_general | solution.py:43
  94.6 0.8 pad_maximum_fusion
  95.5 0.0 reduce-scatter.3.cloned.1.call-update
  95.5 0.0 reduce-scatter.5.cloned.1.call-start
  95.6 0.0 copy-done
  95.6 0.1 dynamic_slice.3
  95.6 6.7 %reduce-scatter.3.cloned.1.call-done = f32[64,1024]{1,0:T(8,128)} async-done(((f32[128,1024]{1,0:T(8,128)}), f32[64,1024]{1,0:T(8,128)}) %reduce-scatter.3.cloned.1.call-update) | async-done | bytes 262160 | tf_op jit(solution)/shard_map/reduce_scatter | solution.py:39
  102.4 1.1 slice_reduce_fusion.1
  103.5 11.9 %all-reduce.1 = (f32[64]{0:T(128)S(1)}, f32[64]{0:T(128)S(1)}) all-reduce(f32[64]{0:T(128)S(1)} %get-tuple-element.6, f32[64]{0:T(128)S(1)} %get-tuple-element.5), channel_id=1, replica_groups=mesh['tok'=4,'hid'=2,'voc'=4] {'voc'}, use_global_device_ids=true, to_apply=%region_6.0 | all-reduce | flops 128 | bytes 1024 | tf_op jit(solution)/shard_map/pmax | solution.py:9
  115.4 1.2 multiply_reduce_fusion
  116.6 8.4 %all-reduce = (f32[64]{0:T(128)S(1)}, f32[64]{0:T(128)S(1)}, f32[64]{0:T(128)S(1)}) all-reduce(f32[64]{0:T(128)S(1)} %get-tuple-element.3, f32[64]{0:T(128)S(1)} %get-tuple-element.4, f32[64]{0:T(128)S(1)} %get-tuple-element.2), channel_id=1, replica_groups=mesh['tok'=4,'hid'=2,'voc'=4] {'voc'}, use_global_device_ids=true, to_apply=%region_8.0 | all-reduce | flops 192 | bytes 1536 | tf_op jit(solution)/shard_map/psum | solution.py:14
  125.0 0.6 add_reduce_fusion
  125.6 1.1 multiply_convert_fusion
  126.7 1.9 %all_gather.15 = bf16[128,512]{1,0:T(8,128)(2,1)S(1)} all-gather(bf16[64,512]{1,0:T(8,128)(2,1)S(1)} %multiply_convert_fusion), channel_id=1, replica_groups=mesh['tok'=4,'hid'=2,'voc'=4] {'hid'}, dimensions={0}, use_global_device_ids=true | all-gather | bytes 196608 | tf_op jit(solution)/shard_map/all_gather | solution.py:58
  128.6 5.0 %fusion.3 = f32[128,4096]{1,0:T(8,128)} fusion(bf16[128,512]{1,0:T(8,128)(2,1)S(1)} %all_gather.15, bf16[4096,512]{1,0:T(8,128)(2,1)} %param.7), kind=kOutput, calls=%fused_computation.13 | convolution fusion | flops 536870912 | bytes 6422528 | tf_op jit(solution)/shard_map/dot_general | solution.py:57
  133.6 0.0 reduce-scatter.5.cloned.1.call-update
  133.6 15.0 %psum.31 = f32[]{:T(128)} all-reduce(f32[]{:T(128)} %get-tuple-element.12), channel_id=1, replica_groups=mesh['tok'=4,'hid'=2,'voc'=4] {'tok','hid'}, use_global_device_ids=true, to_apply=%region_13.0 | all-reduce | flops 1 | bytes 8 | tf_op jit(solution)/shard_map/psum | solution.py:56
  149.2 27.8 %reduce-scatter.5.cloned.1.call-done = f32[128,1024]{1,0:T(8,128)} async-done(((f32[128,4096]{1,0:T(8,128)}), f32[128,1024]{1,0:T(8,128)}) %reduce-scatter.5.cloned.1.call-update) | async-done | bytes 524304 | tf_op jit(solution)/shard_map/reduce_scatter | solution.py:63
  177.0 1.8 convert_element_type.7
Async XLA Ops:
  7.2 33.1 %all-gather.4.cloned.1.call-start = ((), (), s32[]{:S(2)}) async-start(), calls=%async_computation.2 | async-start | bytes 1310720 | tf_op jit(solution)/shard_map/all_gather | solution.py:34
  7.9 79.0 %all-gather.6.cloned.1.call-start = ((), (), s32[]{:S(2)}) async-start(), calls=%async_computation.5 | async-start | bytes 2621440 | tf_op jit(solution)/shard_map/all_gather | solution.py:35
  8.6 93.7 %reduce-scatter.3.cloned.1.call-start = ((), (), s32[]{:S(2)}) async-start(), calls=%async_computation.3 | async-start | bytes 786432 | tf_op jit(solution)/shard_map/reduce_scatter | solution.py:39
  90.0 5.6 %copy-start = (f32[128]{0:T(128)S(1)}, f32[128]{0:T(128)}, u32[]{:S(2)}) copy-start(f32[128]{0:T(128)} %param.9) | copy-start | bytes 1540
  95.5 81.5 %reduce-scatter.5.cloned.1.call-start = ((), (), s32[]{:S(2)}) async-start(), calls=%async_computation.4 | async-start | bytes 2621440 | tf_op jit(solution)/shard_map/reduce_scatter | solution.py:63
Sparse Core Ops, SparseCore 0:
  9.5 30.6 all-gather.3
  41.8 45.0 all-gather.5
  95.6 6.7 reduce-scatter.2
  133.7 43.2 reduce-scatter.4
